TPU v7x, 256 devices: a whole 4x4x8 slice. The times are simulated.
256 devices in a mesh: enc: 8 (over z), bin: 16 (over y_hi, x, core), off: 2 (over y_lo).
Axes of the slice: x: 4, y: 4 (y_hi: 2, y_lo: 2; y = y_hi * 2 + y_lo), z: 8, core: 2. Of those that a mesh axis runs over, the one named last changes fastest.
Arguments:
- encoder_in: bfloat16 [512, 6144], P(('bin', 'off'), 'enc'), may hold values from -6 to 6
- gain_enc: float32 [512], P(('bin', 'off')), may hold values from 0.1 to 1.9
- conv_one: bfloat16 [3, 512, 512], P(None, ('bin', 'off')), may hold values from -0.15625 to 0.15625
- proj_weight: bfloat16 [2, 512, 32], P(None, ('bin', 'off')), may hold values from -0.25 to 0.25
- conv_two: bfloat16 [9, 32, 32], replicated, may hold values from -0.375 to 0.375
- head_weight: float32 [32], replicated, may hold values from -1 to 1
- target: bfloat16 [6144, 2048], P('bin', ('enc', 'off')), may hold values from -8 to 8
- valid_bins: int32 [6144], replicated, may hold values 0 or 1
- offset_limit: int32 [6144], replicated, may hold values from 1024 to 2048
- dilations: int32 [2], replicated, may hold values from 1 to 8, as said below
Outputs:
- prediction: float32 [6144, 2048], P('bin', ('enc', 'off'))
- loss_mean: float32 [1], replicated
- grad_conv_two: float32 [9, 32, 32], replicated
- grad_proj: float32 [2, 512, 32], P(None, ('bin', 'off'))
- grad_conv_one: float32 [3, 512, 512], P(None, ('bin', 'off'), 'enc')
Inputs may be any that keep to these rules, and one draw needn't show every extreme that they name: dilations[0] is the dilation of the 1-D layer and dilations[1] that of the 2-D layer; one of the two equals 8, the other is smaller.
All inputs are finite; a program needn't handle non-finite values.
Results may differ from a plain program's by a relative error of at most 0.0013.
The roundings to bfloat16 on the way count: a program that leaves them out, or rounds other values in their place, can miss the bound.
Values may be sent and summed in bfloat16 or wider, within the bound.
No kernel may reach another device: no remote copies, remote signals or barrier semaphores. Data moves between devices by JAX's collectives and lax.ppermute only.
A program may use at most 192 MiB of HBM per device.

v0:
```python
import jax
import jax.numpy as jnp
from jax import lax
from jax.sharding import PartitionSpec as P

LARGEST_DILATION = 8


def with_halo(cells, sides, width):
    for axis, dim in sides:
        count = lax.axis_size(axis)
        ends = count - 1
        head = lax.slice_in_dim(cells, 0, width, axis=dim)
        tail = lax.slice_in_dim(cells, cells.shape[dim] - width, cells.shape[dim], axis=dim)
        cells = jnp.concatenate(
            [
                lax.ppermute(tail, axis, [(i, (i + 1) % count) for i in range(ends)]),
                cells,
                lax.ppermute(head, axis, [((i + 1) % count, i) for i in range(ends)]),
            ],
            axis=dim,
        )
    return cells


def from_everyone(array, axis):
    size = lax.axis_size(axis)
    return lax.all_to_all(
        jnp.broadcast_to(array[None], (size, *array.shape)), axis, 0, 0, tiled=True
    )


def laid_out(tiles, dim):
    tiles = jnp.moveaxis(tiles, 0, dim)
    shape = tiles.shape
    return tiles.reshape(*shape[:dim], shape[dim] * shape[dim + 1], *shape[dim + 2 :])


def gathered_copies(array, axis, dim):
    tiles = from_everyone(array, axis)
    return laid_out(tiles, dim)


def total_of_pieces(array, axis):
    tiles = lax.all_gather(array, axis)
    return tiles.sum(axis=0)


def of_everyone(array, axis):
    return from_everyone(array, axis).sum(axis=0)


def split_up(array, dim, size):
    shape = array.shape
    tiles = array.reshape(*shape[:dim], size, shape[dim] // size, *shape[dim + 1 :])
    return jnp.moveaxis(tiles, dim, 0)


def sum_at_owner(array, axis, dim):
    size = lax.axis_size(axis)
    tiles = lax.all_to_all(split_up(array, dim, size), axis, 0, 0, tiled=True)
    return jnp.sum(tiles, axis=0)


def hankel(window, tile_rows, tile_cols):
    chans = window.shape[0]
    width = tile_rows + tile_cols
    base = window[:, : width - 1]
    tiled = jnp.broadcast_to(base[:, None, :], (chans, tile_rows, width - 1)).reshape(
        chans, tile_rows * (width - 1)
    )
    tiled = jnp.pad(tiled, ((0, 0), (0, tile_rows)))
    return tiled.reshape(chans, tile_rows, width)[:, :, :tile_cols]


def diagonal_sums(tile):
    chans, tile_rows, tile_cols = tile.shape
    width = tile_rows + tile_cols
    padded_input = jnp.pad(tile, ((0, 0), (0, 0), (0, tile_rows)))
    flat = padded_input.reshape(chans, tile_rows * width)[:, : tile_rows * (width - 1)]
    return jnp.sum(flat.reshape(chans, tile_rows, width - 1), axis=1)


def count_cells(valid_bins, offset_limit):
    sequence_length = valid_bins.shape[0]
    running = jnp.concatenate([jnp.zeros((1,), jnp.int32), jnp.cumsum(valid_bins)])
    places = jnp.arange(sequence_length, dtype=jnp.int32)
    farthest = jnp.minimum(places + offset_limit, sequence_length)
    inside = jnp.take(running, farthest) - jnp.take(running, places)
    return jnp.sum(valid_bins * inside).astype(jnp.float32)


def shards(
    encoder_in,
    gain_enc,
    conv_one,
    proj_weight,
    conv_two,
    head_weight,
    target,
    valid_bins,
    offset_limit,
    dilations,
):
    chans, encoder_bins = encoder_in.shape
    width_in = conv_one.shape[2]
    second_channels = conv_two.shape[1]
    tile_rows, tile_cols = target.shape
    area = tile_rows * tile_cols
    first_dilation = dilations[0]
    second_dilation = dilations[1]
    activ = jax.nn.gelu(gain_enc[:, None] * encoder_in.astype(jnp.float32)).astype(jnp.bfloat16)
    framed = with_halo(activ, (("enc", 1),), LARGEST_DILATION)
    channel_count = gathered_copies(framed, ("bin", "off"), 0)
    stacked_enc = jnp.concatenate(
        [
            lax.dynamic_slice_in_dim(
                channel_count,
                LARGEST_DILATION + (kernel_tap_index - 1) * first_dilation,
                encoder_bins,
                1,
            )
            for kernel_tap_index in range(3)
        ],
        axis=0,
    )
    weight_one = jnp.transpose(conv_one, (1, 0, 2)).reshape(chans, 3 * width_in)
    conv_out = jnp.dot(weight_one, stacked_enc, preferred_element_type=jnp.float32)
    hidden = (encoder_in.astype(jnp.float32) + conv_out).astype(jnp.bfloat16)
    proj_rows = jnp.transpose(proj_weight, (0, 2, 1)).reshape(2 * second_channels, chans)
    partial_embed = jnp.dot(proj_rows, hidden, preferred_element_type=jnp.float32)
    summed = total_of_pieces(partial_embed, ("bin", "off")).astype(jnp.bfloat16)
    embed = gathered_copies(summed, "enc", 1)
    sequence_length = embed.shape[1]
    window_extent = tile_cols * lax.axis_size("enc") * lax.axis_size("off")
    row_start = lax.axis_index("bin") * tile_rows
    offs_start = (lax.axis_index("enc") * lax.axis_size("off") + lax.axis_index("off")) * tile_cols
    near_rows = lax.dynamic_slice_in_dim(embed[:second_channels], row_start, tile_rows, 1)
    far_ext = jnp.concatenate(
        [embed[second_channels:], jnp.zeros((second_channels, window_extent), jnp.bfloat16)], axis=1
    )
    far_window = lax.dynamic_slice_in_dim(far_ext, row_start + offs_start, tile_rows + tile_cols, 1)
    pair_sum = near_rows[:, :, None].astype(jnp.float32) + hankel(
        far_window, tile_rows, tile_cols
    ).astype(jnp.float32)
    band_act = jnp.maximum(pair_sum, 0.0).astype(jnp.bfloat16)
    shifts = [
        (bin_displacement, offset_displacement)
        for bin_displacement in (-1, 0, 1)
        for offset_displacement in (-1, 0, 1)
    ]
    framed_band = with_halo(band_act, (("bin", 1), (("enc", "off"), 2)), LARGEST_DILATION)
    stacked_band = jnp.concatenate(
        [
            lax.dynamic_slice(
                framed_band,
                (
                    0,
                    LARGEST_DILATION + bin_displacement * second_dilation,
                    LARGEST_DILATION + offset_displacement * second_dilation,
                ),
                (second_channels, tile_rows, tile_cols),
            ).reshape(second_channels, area)
            for bin_displacement, offset_displacement in shifts
        ],
        axis=0,
    )
    weight_fwd = jnp.transpose(conv_two, (2, 0, 1)).reshape(second_channels, 9 * second_channels)
    band_conv = jnp.dot(weight_fwd, stacked_band, preferred_element_type=jnp.float32).reshape(
        second_channels, tile_rows, tile_cols
    )
    resid = pair_sum + band_conv
    prediction = jnp.sum(head_weight[:, None, None] * jnp.maximum(resid, 0.0), axis=0)
    mask_float = valid_bins.astype(jnp.float32)
    mask_ext = jnp.concatenate([mask_float, jnp.zeros((window_extent,), jnp.float32)])
    mask_near = lax.dynamic_slice_in_dim(mask_float, row_start, tile_rows)
    mask_far = hankel(
        lax.dynamic_slice_in_dim(mask_ext, row_start + offs_start, tile_rows + tile_cols)[None, :],
        tile_rows,
        tile_cols,
    )[0]
    limit_near = lax.dynamic_slice_in_dim(offset_limit, row_start, tile_rows)
    offs_ids = offs_start + jnp.arange(tile_cols, dtype=jnp.int32)
    weight = (
        mask_near[:, None]
        * mask_far
        * (offs_ids[None, :] < limit_near[:, None]).astype(jnp.float32)
    )
    denom = 1.0 + count_cells(valid_bins, offset_limit)
    differ = prediction - target.astype(jnp.float32)
    error_sum = jnp.sum(weight * differ * differ)
    dpred = 2.0 * weight * differ / denom
    dres = (head_weight[:, None, None] * dpred[None] * (resid > 0.0).astype(jnp.float32)).astype(
        jnp.bfloat16
    )
    grad_band = lax.dot_general(
        stacked_band,
        dres.reshape(second_channels, area),
        (((1,), (1,)), ((), ())),
        preferred_element_type=jnp.float32,
    ).reshape(9, second_channels, second_channels)
    framed_grad = with_halo(dres, (("bin", 1), (("enc", "off"), 2)), LARGEST_DILATION)
    stacked_grad = jnp.concatenate(
        [
            lax.dynamic_slice(
                framed_grad,
                (
                    0,
                    LARGEST_DILATION - bin_displacement * second_dilation,
                    LARGEST_DILATION - offset_displacement * second_dilation,
                ),
                (second_channels, tile_rows, tile_cols),
            ).reshape(second_channels, area)
            for bin_displacement, offset_displacement in shifts
        ],
        axis=0,
    )
    weight_back = jnp.transpose(conv_two, (1, 0, 2)).reshape(second_channels, 9 * second_channels)
    dact = jnp.dot(weight_back, stacked_grad, preferred_element_type=jnp.float32).reshape(
        second_channels, tile_rows, tile_cols
    )
    dpair = dres.astype(jnp.float32) + dact * (pair_sum > 0.0).astype(jnp.float32)
    near_grad = jnp.sum(dpair, axis=2)
    far_grad = diagonal_sums(dpair)
    enc_start = lax.axis_index("enc") * encoder_bins
    buffer = jnp.zeros((2, second_channels, sequence_length + window_extent), jnp.float32)
    buffer = lax.dynamic_update_slice(buffer, near_grad[None], (0, 0, row_start))
    buffer = lax.dynamic_update_slice(buffer, far_grad[None], (1, 0, row_start + offs_start))
    buffer = buffer[:, :, :sequence_length]
    grad_whole, grad_conv_two, total_error = lax.psum(
        (buffer, grad_band, error_sum), ("enc", "bin", "off")
    )
    grad_embed = lax.dynamic_slice_in_dim(grad_whole, enc_start, encoder_bins, 2).astype(
        jnp.bfloat16
    )
    grad_rows = grad_embed.reshape(2 * second_channels, encoder_bins)
    dhidden = jnp.dot(proj_rows.T, grad_rows, preferred_element_type=jnp.float32).astype(
        jnp.bfloat16
    )
    proj_local = jnp.dot(hidden, grad_rows.T, preferred_element_type=jnp.float32)
    proj_local = jnp.transpose(proj_local.reshape(chans, 2, second_channels), (1, 0, 2))
    conv_local = lax.dot_general(
        dhidden, stacked_enc, (((1,), (1,)), ((), ())), preferred_element_type=jnp.float32
    )
    conv_local = jnp.transpose(conv_local.reshape(chans, 3, width_in), (1, 0, 2))
    grad_proj = of_everyone(proj_local, "enc")
    grad_conv_one = sum_at_owner(conv_local, "enc", 2)
    loss_mean = (total_error / denom).reshape(1)
    return (prediction, loss_mean, grad_conv_two, grad_proj, grad_conv_one)


def solution(mesh):
    in_specs = (
        P(("bin", "off"), "enc"),
        P(("bin", "off")),
        P(None, ("bin", "off"), None),
        P(None, ("bin", "off"), None),
        P(),
        P(),
        P("bin", ("enc", "off")),
        P(),
        P(),
        P(),
    )
    out_specs = (
        P("bin", ("enc", "off")),
        P(),
        P(),
        P(None, ("bin", "off"), None),
        P(None, ("bin", "off"), "enc"),
    )
    return jax.shard_map(shards, mesh=mesh, in_specs=in_specs, out_specs=out_specs, check_vma=False)
```

profile of v0, /device:TPU:32, one launch (start us, length us, event | category | flops | bytes accessed | tf_op | source)
XLA Modules:
  0.0 812.7 jit_solution(11922956676529906253)
XLA Ops:
  8.2 3.7 collective-permute-start.1
  14.0 3.4 collective-permute-done
  18.5 5.6 all-to-all-start
  29.0 11.5 %all-to-all-done = bf16[32,16,784]{2,1,0:T(8,128)(2,1)S(1)} async-done(((bf16[32,16,784]{2,1,0:T(8,128)(2,1)}), bf16[32,16,784]{2,1,0:T(8,128)(2,1)S(1)}, u32[]{:S(2)}, u32[]{:S(2)}) %all-to-all-start) | async-done | bytes 802848 | tf_op jit(solution)/shard_map/all_to_all | solution.py:28
  44.6 91.0 %all-gather.3.cloned.1.call-done = f32[2048,768]{1,0:T(8,128)} async-done(((f32[64,768]{1,0:T(8,128)}), f32[2048,768]{1,0:T(8,128)}) %all-gather.3.cloned.1.call-update) | async-done | bytes 6291472 | tf_op jit(solution)/shard_map/all_gather | solution.py:45
  139.6 7.5 all-to-all-start.1
  147.9 34.3 %gather_fusion.1 = s32[6144]{0:T(1024)S(1)} fusion(s32[6145]{0:T(1024)S(1)} %pad_add_fusion, s32[6144]{0:T(1024)S(1)} %get-tuple-element.63), kind=kCustom, calls=%fused_computation.1.clone | custom fusion | bytes 73728 | tf_op jit(solution)/shard_map/jit(_take)/gather | solution.py:89
  182.2 34.3 %gather_fusion = s32[6144]{0:T(1024)S(1)} fusion(s32[6145]{0:T(1024)S(1)} %pad_add_fusion, s32[6144]{0:T(1024)S(1)} %get-tuple-element.64), kind=kCustom, calls=%fused_computation.clone | custom fusion | bytes 73728 | tf_op jit(solution)/shard_map/jit(_take)/gather | solution.py:89
  216.7 5.5 broadcast_in_dim.30
  222.2 21.4 %reshape.201 = bf16[32,196224]{1,0:T(8,128)(2,1)} reshape(bf16[32,384,511]{2,1,0:T(8,128)(2,1)} %broadcast_in_dim.30) | data formatting | bytes 25116672 | tf_op jit(solution)/shard_map/reshape | solution.py:69
  243.6 6.1 pad.14
  249.7 11.2 %copy.122 = bf16[4,8,384,512]{3,2,1,0:T(8,128)(2,1)S(1)} copy(bf16[4,8,384,512]{3,1,2,0:T(8,128)(2,1)S(1)} %bitcast.171) | data formatting | bytes 25165824
  261.0 4.4 copy-done.1
  272.9 3.9 fusion.30
  276.7 4.0 copy.102
  284.0 4.0 copy.101
  295.9 3.4 broadcast_in_dim.34
  299.3 10.0 %pad_reduce_fusion = f32[196608]{0:T(1024)} fusion(f32[1,196224]{1,0:T(1,128)} %broadcast_in_dim.34), kind=kLoop, calls=%fused_computation.43 | loop fusion | bytes 1571328 | tf_op jit(solution)/shard_map/jit(_pad)/pad | solution.py:72
  315.4 3.6 copy.104
  319.1 3.7 copy.103
  322.7 8.9 %pad_maximum_fusion = bf16[32,400,144]{2,1,0:T(8,128)(2,1)} fusion(bf16[32,400,8]{2,1,0:T(8,128)(2,1)} %copy.104, bf16[32,8,128]{2,1,0:T(8,128)(2,1)S(1)} %collective-permute-done.3, bf16[32,384,128]{2,1,0:T(8,128)(2,1)S(1)} %maximum_convert_fusion, bf16[32,8,128]{2,1,0:T(8,128)(2,1)} %copy-done.24, bf16[32,400,8]{2,1,0:T(8,128)(2,1)} %copy.103), kind=kLoop, calls=%fused_computation.2 | loop fusion | flops 18432000 | bytes 7372800 | tf_op jit(solution)/shard_map/concatenate | solution.py:15
  331.7 37.3 %constant_dynamic-slice_fusion.8 = (bf16[32,384,128]{2,1,0:T(8,128)(2,1)}, bf16[32,384,128]{2,1,0:T(8,128)(2,1)}, bf16[32,384,128]{2,1,0:T(8,128)(2,1)}, bf16[32...) fusion(bf16[32,400,144]{2,1,0:T(8,128)(2,1)} %pad_maximum_fusio, ...), kind=kLoop, calls=%fused_computation.89 | loop fusion | bytes 50331664 | tf_op jit(solution)/shard_map/dynamic_slice | solution.py:155
  369.0 5.5 bitcast_dynamic-update-slice_fusion.17
  374.5 3.5 bitcast_dynamic-update-slice_fusion.16
  378.0 3.6 bitcast_dynamic-update-slice_fusion.15
  381.6 3.5 bitcast_dynamic-update-slice_fusion.14
  385.1 3.5 bitcast_dynamic-update-slice_fusion.13
  388.6 3.5 bitcast_dynamic-update-slice_fusion.12
  392.0 3.9 bitcast_dynamic-update-slice_fusion.11
  396.0 3.5 bitcast_dynamic-update-slice_fusion.10
  399.5 3.5 bitcast_dynamic-update-slice_fusion.9
  403.0 11.8 %convolution_bitcast_fusion.1 = f32[4,8,384,128]{3,1,2,0:T(8,128)S(1)} fusion(bf16[288,49152]{1,0:T(8,128)(2,1)} %bitcast_dynamic-update-slice_fusion.9, bf16[32,288]{0,1:T(8,128)(2,1)S(1)} %bitcast.195), kind=kOutput, calls=%fused_computation.33 | convolution fusion | flops 905969664 | bytes 34621440 | tf_op jit(solution)/shard_map/dot_general | solution.py:169
  418.7 4.1 multiply_reduce_fusion
  424.6 5.2 select_convert_fusion
  431.8 3.5 collective-permute-start.6
  440.6 3.9 fusion.29
  444.5 4.0 copy.110
  448.5 3.8 collective-permute-start.9
  452.3 4.0 copy.109
  458.6 14.4 %fusion.35 = f32[9,32,32]{2,1,0:T(8,128)} fusion(bf16[9,32,49152]{2,1,0:T(8,128)(2,1)} %bitcast.26, bf16[32,49152,1]{1,0,2:T(8,128)(2,1)} %reshape.256), kind=kOutput, calls=%fused_computation.110 | convolution fusion | flops 905969664 | bytes 31494144 | tf_op jit(solution)/shard_map/dot_general | solution.py:196
  473.0 3.6 copy.112
  476.7 3.7 copy.111
  480.4 8.9 %pad_maximum_fusion.1 = bf16[32,400,144]{2,1,0:T(8,128)(2,1)} fusion(bf16[32,400,8]{2,1,0:T(8,128)(2,1)} %copy.112, bf16[32,8,128]{2,1,0:T(8,128)(2,1)S(1)} %collective-permute-done.7, bf16[32,384,128]{2,1,0:T(8,128)(2,1)S(1)} %select_convert_fusion, bf16[32,8,128]{2,1,0:T(8,128)(2,1)S(1)} %collective-permute-done.6, bf16[32,400,8]{2,1,0:T(8,128)(2,1)} %copy.111), kind=kLoop, calls=%fused_computation.3 | loop fusion | flops 18432000 | bytes 7372800 | tf_op jit(solution)/shard_map/concatenate | solution.py:15
  489.3 37.6 %constant_dynamic-slice_fusion = (bf16[32,384,128]{2,1,0:T(8,128)(2,1)}, bf16[32,384,128]{2,1,0:T(8,128)(2,1)}, bf16[32,384,128]{2,1,0:T(8,128)(2,1)}, bf16[32,3...) fusion(bf16[32,400,144]{2,1,0:T(8,128)(2,1)} %pad_maximum_fusio, ...), kind=kLoop, calls=%fused_computation.81 | loop fusion | bytes 50331664 | tf_op jit(solution)/shard_map/dynamic_slice | solution.py:205
  526.9 5.5 bitcast_dynamic-update-slice_fusion.8
  532.4 3.5 bitcast_dynamic-update-slice_fusion.7
  535.9 3.6 bitcast_dynamic-update-slice_fusion.6
  539.4 3.5 bitcast_dynamic-update-slice_fusion.5
  542.9 3.5 bitcast_dynamic-update-slice_fusion.4
  546.4 3.5 bitcast_dynamic-update-slice_fusion.3
  549.9 3.7 bitcast_dynamic-update-slice_fusion.2
  553.6 3.5 bitcast_dynamic-update-slice_fusion.1
  557.1 3.5 bitcast_dynamic-update-slice_fusion
  560.6 11.8 %convolution_bitcast_fusion = f32[4,8,384,128]{3,1,2,0:T(8,128)S(1)} fusion(bf16[288,49152]{1,0:T(8,128)(2,1)} %bitcast_dynamic-update-slice_fusion, bf16[32,288]{0,1:T(8,128)(2,1)S(1)} %bitcast.197), kind=kOutput, calls=%fused_computation.32 | convolution fusion | flops 905969664 | bytes 34621440 | tf_op jit(solution)/shard_map/dot_general | solution.py:219
  573.6 6.9 fusion.27
  580.4 14.4 %pad.16 = f32[32,384,512]{2,1,0:T(8,128)} pad(f32[32,384,128]{2,1,0:T(8,128)} %get-tuple-element.25, f32[]{:T(128)} %constant.90.clone.1), padding=0_0x0_0x0_384 | pad | bytes 31457284 | tf_op jit(solution)/shard_map/jit(_pad)/pad | solution.py:79
  594.8 22.0 %copy.143 = f32[4,8,384,512]{3,1,2,0:T(8,128)S(1)} copy(f32[4,8,384,512]{3,2,1,0:T(8,128)} %bitcast.164) | data formatting | bytes 50331648
  616.8 8.6 %slice.118 = f32[32,196224]{1,0:T(8,128)} slice(f32[32,196608]{1,0:T(8,128)S(1)} %bitcast.165), slice={[0:32], [0:196224]} | slice | bytes 50233344 | tf_op jit(solution)/shard_map/slice | solution.py:80
  625.4 43.9 %reshape.230 = f32[32,384,511]{2,1,0:T(8,128)} reshape(f32[32,196224]{1,0:T(8,128)} %slice.118) | data formatting | bytes 50233344 | tf_op jit(solution)/shard_map/reshape | solution.py:81
  669.3 10.0 %reduce_sum.77 = f32[32,511]{1,0:T(8,128)S(1)} reduce(f32[32,384,511]{2,1,0:T(8,128)} %reshape.230, f32[]{:T(128)} %constant.90.clone.1), dimensions={1}, to_apply=%region_9.11 | reduce | flops 6262816 | bytes 25182084 | tf_op jit(solution)/shard_map/reduce_sum | solution.py:81
  681.5 93.5 %all-reduce.7 = (f32[]{:T(128)}, f32[9,32,32]{2,1,0:T(8,128)}, bf16[2,32,6144]{2,1,0:T(8,128)(2,1)S(1)}) all-reduce(f32[]{:T(128)} %get-tuple-element.56, f32[9,32,32]{2,1,0:T(8,128)S(1)} %copy-done.25, f32[2,32,6144]{2,1,0:T(8,128)} %slice.119), channel_id=1, replica_groups=mesh['enc'=8,'bin'=16,'off'=2] {'enc','bin','off'}, use_global_device_ids=true, to_apply=%region_3.4 | all-reduce | flops 402433 | bytes 2433032 | tf_op jit(solution)/shard_map/psum | solution.py:230
  776.0 8.2 %all-to-all-start.2 = ((f32[8,1,1024]{2,1,0:T(1,128)}), f32[8,1,1024]{2,1,0:T(1,128)S(1)}, u32[]{:S(2)}, u32[]{:S(2)}) async-start(f32[8,1,1024]{2,1,0:T(1,128)} %reshape.268), calls=%async_computation.2 | async-start | bytes 65536 | tf_op jit(solution)/shard_map/all_to_all | solution.py:28
  790.7 4.7 all-to-all-start.3
  798.1 4.7 all-to-all-done.3
  (158 shorter events, 65.4 us)
Async XLA Ops:
  7.2 35.5 %copy-start.30 = (bf16[16,768]{1,0:T(8,128)(2,1)S(1)}, bf16[16,768]{1,0:T(8,128)(2,1)}, u32[]{:S(2)}) copy-start(bf16[16,768]{1,0:T(8,128)(2,1)} %param.12) | copy-start | bytes 73732
  8.2 5.8 collective-permute-start.1
  11.9 5.5 collective-permute-start
  18.5 22.0 %all-to-all-start = ((bf16[32,16,784]{2,1,0:T(8,128)(2,1)}), bf16[32,16,784]{2,1,0:T(8,128)(2,1)S(1)}, u32[]{:S(2)}, u32[]{:S(2)}) async-start(bf16[32,16,784]{2,1,0:T(8,128)(2,1)} %broadcast_in_dim.26), calls=%async_computation | async-start | bytes 1835008 | tf_op jit(solution)/shard_map/all_to_all | solution.py:28
  24.1 111.5 %all-gather.3.cloned.1.call-start = ((), (), s32[]{:S(2)}) async-start(), calls=%async_computation.4 | async-start | bytes 6488064 | tf_op jit(solution)/shard_map/all_gather | solution.py:45
  41.7 0.9 copy-start.16
  41.7 1.3 copy-start.18
  41.7 1.4 copy-start.19
  42.6 104.5 %copy-start.29 = (s32[6144]{0:T(1024)S(1)}, s32[6144]{0:T(1024)}, u32[]{:S(2)}) copy-start(s32[6144]{0:T(1024)} %param.19) | copy-start | bytes 73732
  42.6 105.2 %copy-start.26 = (s32[6144]{0:T(1024)S(1)}, s32[6144]{0:T(1024)}, u32[]{:S(2)}) copy-start(s32[6144]{0:T(1024)} %param.20) | copy-start | bytes 73732
  43.1 0.6 copy-start.27
  139.6 76.8 %all-to-all-start.1 = ((bf16[8,64,768]{2,1,0:T(8,128)(2,1)}), bf16[8,64,768]{2,1,0:T(8,128)(2,1)S(1)}, u32[]{:S(2)}, u32[]{:S(2)}) async-start(bf16[8,64,768]{2,1,0:T(8,128)(2,1)} %broadcast_in_dim.27), calls=%async_computation.1 | async-start | bytes 1572864 | tf_op jit(solution)/shard_map/all_to_all | solution.py:28
  260.9 4.5 copy-start.1
  267.4 5.1 collective-permute-start.3
  268.7 3.9 collective-permute-start.2
  272.6 4.1 copy-start.24
  280.7 34.7 %collective-permute-start.5 = (bf16[32,400,8]{1,2,0:T(8,128)(2,1)}, bf16[32,400,8]{1,2,0:T(8,128)(2,1)}, u32[]{:S(2)}, u32[]{:S(2)}) collective-permute-start(bf16[32,400,8]{1,2,0:T(8,128)(2,1)} %copy.102), channel_id=1, source_target_pairs={{1,0},{32,1},{33,32},{64,33},{65,64},{96,65},{97,96},{128,97},{129... | collective-permute-start | bytes 614408 | tf_op jit(solution)/shard_map/ppermute | solution.py:19
  287.9 31.1 %collective-permute-start.4 = (bf16[32,400,8]{1,2,0:T(8,128)(2,1)}, bf16[32,400,8]{1,2,0:T(8,128)(2,1)}, u32[]{:S(2)}, u32[]{:S(2)}) collective-permute-start(bf16[32,400,8]{1,2,0:T(8,128)(2,1)} %copy.101), channel_id=1, source_target_pairs={{0,1},{1,32},{32,33},{33,64},{64,65},{65,96},{96,97},{97,128},{128... | collective-permute-start | bytes 614408 | tf_op jit(solution)/shard_map/ppermute | solution.py:17
  369.0 5.5 copy-start.14
  369.0 9.0 %copy-start.12 = (bf16[32,384,128]{2,1,0:T(8,128)(2,1)S(1)}, bf16[32,384,128]{2,1,0:T(8,128)(2,1)}, u32[]{:S(2)}) copy-start(bf16[32,384,128]{2,1,0:T(8,128)(2,1)} %get-tuple-element.39) | copy-start | bytes 9437188
  374.5 7.1 copy-start.10
  381.6 7.0 copy-start.8
  385.1 7.0 copy-start.6
  388.6 7.4 copy-start.4
  392.0 7.5 copy-start.2
  396.0 7.0 copy-start.22
  414.8 3.9 copy-start.34
  416.0 2.7 copy-start
  418.7 4.3 copy-start.20
  418.7 4.3 copy-start.31
  418.7 4.3 copy-start.32
  418.7 4.3 copy-start.35
  422.8 7.0 copy-start.21
  424.6 12.6 %copy-start.23 = (bf16[9,32,32]{2,1,0:T(8,128)(2,1)S(1)}, bf16[9,32,32]{2,1,0:T(8,128)(2,1)}, u32[]{:S(2)}) copy-start(bf16[9,32,32]{2,1,0:T(8,128)(2,1)} %param.16) | copy-start | bytes 55300
  430.5 9.9 %collective-permute-start.7 = (bf16[32,8,128]{2,1,0:T(8,128)(2,1)}, bf16[32,8,128]{2,1,0:T(8,128)(2,1)S(1)}, u32[]{:S(2)}, u32[]{:S(2)}) collective-permute-start(bf16[32,8,128]{2,1,0:T(8,128)(2,1)} %get-tuple-element.47), channel_id=1, source_target_pairs={{2,0},{4,2},{6,4},{8,6},{10,8},{12,10},{14,12},{16,14},{18,16},{20... | collective-permute-start | bytes 196616 | tf_op jit(solution)/shard_map/ppermute | solution.py:19
  431.8 8.6 %collective-permute-start.6 = (bf16[32,8,128]{2,1,0:T(8,128)(2,1)}, bf16[32,8,128]{2,1,0:T(8,128)(2,1)S(1)}, u32[]{:S(2)}, u32[]{:S(2)}) collective-permute-start(bf16[32,8,128]{2,1,0:T(8,128)(2,1)} %get-tuple-element.46), channel_id=1, source_target_pairs={{0,2},{2,4},{4,6},{6,8},{8,10},{10,12},{12,14},{14,16},{16,18},{18... | collective-permute-start | bytes 196616 | tf_op jit(solution)/shard_map/ppermute | solution.py:17
  448.5 24.6 %collective-permute-start.9 = (bf16[32,400,8]{1,2,0:T(8,128)(2,1)}, bf16[32,400,8]{1,2,0:T(8,128)(2,1)}, u32[]{:S(2)}, u32[]{:S(2)}) collective-permute-start(bf16[32,400,8]{1,2,0:T(8,128)(2,1)} %copy.110), channel_id=1, source_target_pairs={{1,0},{32,1},{33,32},{64,33},{65,64},{96,65},{97,96},{128,97},{129... | collective-permute-start | bytes 614408 | tf_op jit(solution)/shard_map/ppermute | solution.py:19
  456.2 20.5 %collective-permute-start.8 = (bf16[32,400,8]{1,2,0:T(8,128)(2,1)}, bf16[32,400,8]{1,2,0:T(8,128)(2,1)}, u32[]{:S(2)}, u32[]{:S(2)}) collective-permute-start(bf16[32,400,8]{1,2,0:T(8,128)(2,1)} %copy.109), channel_id=1, source_target_pairs={{0,1},{1,32},{32,33},{33,64},{64,65},{65,96},{96,97},{97,128},{128... | collective-permute-start | bytes 614408 | tf_op jit(solution)/shard_map/ppermute | solution.py:17
  526.9 5.5 copy-start.15
  526.9 9.0 %copy-start.13 = (bf16[32,384,128]{2,1,0:T(8,128)(2,1)S(1)}, bf16[32,384,128]{2,1,0:T(8,128)(2,1)}, u32[]{:S(2)}) copy-start(bf16[32,384,128]{2,1,0:T(8,128)(2,1)} %get-tuple-element.31) | copy-start | bytes 9437188
  532.4 7.1 copy-start.11
  539.4 7.0 copy-start.9
  542.9 7.0 copy-start.7
  546.4 7.2 copy-start.5
  549.9 7.2 copy-start.3
  669.3 12.2 %copy-start.25 = (f32[9,32,32]{2,1,0:T(8,128)S(1)}, f32[9,32,32]{2,1,0:T(8,128)}, u32[]{:S(2)}) copy-start(f32[9,32,32]{2,1,0:T(8,128)} %fusion.35) | copy-start | bytes 110596
  679.3 95.7 %copy-start.28 = (bf16[16,768]{1,0:T(8,128)(2,1)S(1)}, bf16[16,768]{1,0:T(8,128)(2,1)}, u32[]{:S(2)}) copy-start(bf16[16,768]{1,0:T(8,128)(2,1)} %copy-done.27) | copy-start | bytes 73732
  679.4 104.8 %copy-start.17 = (bf16[512,768]{1,0:T(8,128)(2,1)S(1)}, bf16[512,768]{1,0:T(8,128)(2,1)}, u32[]{:S(2)}) copy-start(bf16[512,768]{1,0:T(8,128)(2,1)} %copy-done.16) | copy-start | bytes 2359300
  679.4 104.8 %copy-start.33 = (bf16[2,16,32]{2,1,0:T(8,128)(2,1)S(1)}, bf16[2,16,32]{2,1,0:T(8,128)(2,1)}, u32[]{:S(2)}) copy-start(bf16[2,16,32]{2,1,0:T(8,128)(2,1)} %param.15) | copy-start | bytes 6148
  776.0 14.7 %all-to-all-start.2 = ((f32[8,1,1024]{2,1,0:T(1,128)}), f32[8,1,1024]{2,1,0:T(1,128)S(1)}, u32[]{:S(2)}, u32[]{:S(2)}) async-start(f32[8,1,1024]{2,1,0:T(1,128)} %reshape.268), calls=%async_computation.2 | async-start | bytes 65536 | tf_op jit(solution)/shard_map/all_to_all | solution.py:28
  790.7 12.0 %all-to-all-start.3 = ((f32[8,1,3072]{2,1,0:T(1,128)}), f32[8,1,3072]{2,1,0:T(1,128)S(1)}, u32[]{:S(2)}, u32[]{:S(2)}) async-start(f32[8,1,3072]{2,1,0:T(1,128)} %reshape.270), calls=%async_computation.3 | async-start | bytes 196608 | tf_op jit(solution)/shard_map/all_to_all | solution.py:61
Sparse Core Ops, SparseCore 0:
  44.8 90.7 all-gather.2
where the time goes:
time: 823 us; the launch traced here: 813 us
  local copies, waits for them, and re-layouts  430 us (52%)
  waiting for transfers between devices  114 us (14%)
  blocking collectives  93.5 us (11%)
  other arithmetic  56 us (7%)
  starting transfers between devices  53.5 us (7%)
  matrix products  41.6 us (5%)
  between operations  24 us (3%)
    unnamed x100, local copies, waits for them, and re-layouts  109 us
    psum x1, blocking collectives, shards(): lax.psum((buffer, grad_band, error_sum), ('enc', 'bin', 'off'))  93.5 us
    all_gather x1, waiting for transfers between devices, total_of_pieces(): tiles = lax.all_gather(array, axis)  91 us
    gather x2, local copies, waits for them, and re-layouts, count_cells(): inside = jnp.take(running, farthest) - jnp.take(running, places)  68.6 us
    reshape x1, local copies, waits for them, and re-layouts, diagonal_sums(): return jnp.sum(flat.reshape(chans, tile_rows, width - 1), axis=1)  43.9 us
    dynamic_slice x1, local copies, waits for them, and re-layouts, shards(): lax.dynamic_slice(framed_grad, (0, LARGEST_DILATION - bin_displacement *...  37.6 us
    dynamic_slice x1, local copies, waits for them, and re-layouts, shards(): lax.dynamic_slice(framed_band, (0, LARGEST_DILATION + bin_displacement *...  37.3 us
    reshape x1, local copies, waits for them, and re-layouts, hankel(): jnp.broadcast_to(base[:, None, :], (chans, tile_rows, width - 1))  21.4 us
  transfers between devices with their start and end apart: 15, of which 6 were waited for; matrix products, arithmetic and copies ran while one was open for 16% of the time, Pallas kernels for 0%

commit v1 on v0

--- a/solution.py
+++ b/solution.py
@@ -228,7 +228,7 @@
     buffer = lax.dynamic_update_slice(buffer, far_grad[None], (1, 0, row_start + offs_start))
     buffer = buffer[:, :, :sequence_length]
     grad_whole, grad_conv_two, total_error = lax.psum(
-        (buffer, grad_band, error_sum), ("enc", "bin", "off")
+        lax.psum((buffer, grad_band, error_sum), ("bin", "off")), "enc"
     )
     grad_embed = lax.dynamic_slice_in_dim(grad_whole, enc_start, encoder_bins, 2).astype(
         jnp.bfloat16

time: 823 us -> 926 us (1.13)
  blocking collectives: 93.5 us -> 199 us
    psum x1 -> x2, blocking collectives: 93.5 us -> 199 us  [the longest x1 133 us: shards(): lax.psum((buffer, grad_band, error_sum), ('bin', 'off'))]
    unnamed x100 -> x102, local copies, waits for them, and re-layouts: 109 us -> 109 us
  transfers between devices with their start and end apart: 15 -> 16, of which waited for: 6 -> 7; matrix products, arithmetic and copies ran while one was open for 16% -> 14% of each run, Pallas kernels for 0% -> 0%
where the time goes in v1:
time: 926 us; the launch traced here: 915 us
  local copies, waits for them, and re-layouts  430 us (46%)
  blocking collectives  199 us (21%)
  waiting for transfers between devices  116 us (13%)
  other arithmetic  55.8 us (6%)
  starting transfers between devices  50.7 us (5%)
  matrix products  39.4 us (4%)
  between operations  23.9 us (3%)
    psum x1, blocking collectives, shards(): lax.psum((buffer, grad_band, error_sum), ('bin', 'off'))  133 us
    unnamed x102, local copies, waits for them, and re-layouts  109 us
    all_gather x1, waiting for transfers between devices, total_of_pieces(): tiles = lax.all_gather(array, axis)  91 us
    gather x2, local copies, waits for them, and re-layouts, count_cells(): inside = jnp.take(running, farthest) - jnp.take(running, places)  68.6 us
    psum x1, blocking collectives, shards(): lax.psum(lax.psum((buffer, grad_band, error_sum), ('bin', 'off')), 'enc')  66.4 us
    reshape x1, local copies, waits for them, and re-layouts, diagonal_sums(): return jnp.sum(flat.reshape(chans, tile_rows, width - 1), axis=1)  43.9 us
    dynamic_slice x1, local copies, waits for them, and re-layouts, shards(): lax.dynamic_slice(framed_band, (0, LARGEST_DILATION + bin_displacement *...  37.8 us
    dynamic_slice x1, local copies, waits for them, and re-layouts, shards(): lax.dynamic_slice(framed_grad, (0, LARGEST_DILATION - bin_displacement *...  37 us
  transfers between devices with their start and end apart: 16, of which 7 were waited for; matrix products, arithmetic and copies ran while one was open for 14% of the time, Pallas kernels for 0%

profile of v1, /device:TPU:32, one launch (start us, length us, event | category | flops | bytes accessed | tf_op | source)
XLA Modules:
  0.0 915.1 jit_solution(6404339085741249478)
XLA Ops:
  8.2 3.7 collective-permute-start.1
  18.5 5.6 all-to-all-start
  29.0 11.5 %all-to-all-done = bf16[32,16,784]{2,1,0:T(8,128)(2,1)S(1)} async-done(((bf16[32,16,784]{2,1,0:T(8,128)(2,1)}), bf16[32,16,784]{2,1,0:T(8,128)(2,1)S(1)}, u32[]{:S(2)}, u32[]{:S(2)}) %all-to-all-start) | async-done | bytes 802848 | tf_op jit(solution)/shard_map/all_to_all | solution.py:28
  44.7 91.0 %all-gather.3.cloned.1.call-done = f32[2048,768]{1,0:T(8,128)} async-done(((f32[64,768]{1,0:T(8,128)}), f32[2048,768]{1,0:T(8,128)}) %all-gather.3.cloned.1.call-update) | async-done | bytes 6291472 | tf_op jit(solution)/shard_map/all_gather | solution.py:45
  139.7 7.5 all-to-all-start.1
  147.9 34.3 %gather_fusion.1 = s32[6144]{0:T(1024)S(1)} fusion(s32[6145]{0:T(1024)S(1)} %pad_add_fusion, s32[6144]{0:T(1024)S(1)} %get-tuple-element.65), kind=kCustom, calls=%fused_computation.1.clone | custom fusion | bytes 73728 | tf_op jit(solution)/shard_map/jit(_take)/gather | solution.py:89
  182.2 34.3 %gather_fusion = s32[6144]{0:T(1024)S(1)} fusion(s32[6145]{0:T(1024)S(1)} %pad_add_fusion, s32[6144]{0:T(1024)S(1)} %get-tuple-element.66), kind=kCustom, calls=%fused_computation.clone | custom fusion | bytes 73728 | tf_op jit(solution)/shard_map/jit(_take)/gather | solution.py:89
  216.7 5.6 broadcast_in_dim.30
  222.3 21.4 %reshape.201 = bf16[32,196224]{1,0:T(8,128)(2,1)} reshape(bf16[32,384,511]{2,1,0:T(8,128)(2,1)} %broadcast_in_dim.30) | data formatting | bytes 25116672 | tf_op jit(solution)/shard_map/reshape | solution.py:69
  243.7 6.1 pad.14
  249.8 11.2 %copy.122 = bf16[4,8,384,512]{3,2,1,0:T(8,128)(2,1)S(1)} copy(bf16[4,8,384,512]{3,1,2,0:T(8,128)(2,1)S(1)} %bitcast.171) | data formatting | bytes 25165824
  261.1 4.5 copy-done.1
  273.1 3.8 fusion.30
  276.9 4.0 copy.102
  284.2 4.0 copy.101
  299.5 10.0 %pad_reduce_fusion = f32[196608]{0:T(1024)} fusion(f32[1,196224]{1,0:T(1,128)} %broadcast_in_dim.34), kind=kLoop, calls=%fused_computation.43 | loop fusion | bytes 1571328 | tf_op jit(solution)/shard_map/jit(_pad)/pad | solution.py:72
  315.6 3.7 copy.104
  319.3 3.7 copy.103
  323.1 8.9 pad_maximum_fusion
  332.0 37.8 %constant_dynamic-slice_fusion.8 = (bf16[32,384,128]{2,1,0:T(8,128)(2,1)}, bf16[32,384,128]{2,1,0:T(8,128)(2,1)}, bf16[32,384,128]{2,1,0:T(8,128)(2,1)}, bf16[32...) fusion(bf16[32,400,144]{2,1,0:T(8,128)(2,1)} %pad_maximum_fusio, ...), kind=kLoop, calls=%fused_computation.89 | loop fusion | bytes 50331664 | tf_op jit(solution)/shard_map/dynamic_slice | solution.py:155
  369.8 5.5 bitcast_dynamic-update-slice_fusion.17
  375.3 3.5 bitcast_dynamic-update-slice_fusion.16
  378.8 3.5 bitcast_dynamic-update-slice_fusion.15
  382.3 3.6 bitcast_dynamic-update-slice_fusion.14
  385.9 3.6 bitcast_dynamic-update-slice_fusion.13
  389.4 3.5 bitcast_dynamic-update-slice_fusion.12
  392.9 3.9 bitcast_dynamic-update-slice_fusion.11
  396.8 3.5 bitcast_dynamic-update-slice_fusion.10
  400.3 3.5 bitcast_dynamic-update-slice_fusion.9
  403.8 11.8 %convolution_bitcast_fusion.1 = f32[4,8,384,128]{3,1,2,0:T(8,128)S(1)} fusion(bf16[288,49152]{1,0:T(8,128)(2,1)} %bitcast_dynamic-update-slice_fusion.9, bf16[32,288]{0,1:T(8,128)(2,1)S(1)} %bitcast.195), kind=kOutput, calls=%fused_computation.33 | convolution fusion | flops 905969664 | bytes 34621440 | tf_op jit(solution)/shard_map/dot_general | solution.py:169
  419.3 4.1 multiply_reduce_fusion
  425.2 5.2 select_convert_fusion
  431.8 3.5 collective-permute-start.6
  436.4 3.8 fusion.29
  440.2 4.1 copy.110
  444.3 3.9 collective-permute-start.9
  448.2 4.0 copy.109
  459.4 3.7 copy.112
  463.1 3.7 copy.111
  466.8 8.8 pad_maximum_fusion.1
  475.6 37.0 %constant_dynamic-slice_fusion = (bf16[32,384,128]{2,1,0:T(8,128)(2,1)}, bf16[32,384,128]{2,1,0:T(8,128)(2,1)}, bf16[32,384,128]{2,1,0:T(8,128)(2,1)}, bf16[32,3...) fusion(bf16[32,400,144]{2,1,0:T(8,128)(2,1)} %pad_maximum_fusio, ...), kind=kLoop, calls=%fused_computation.81 | loop fusion | bytes 50331664 | tf_op jit(solution)/shard_map/dynamic_slice | solution.py:205
  512.6 5.5 bitcast_dynamic-update-slice_fusion.8
  518.1 3.5 bitcast_dynamic-update-slice_fusion.7
  521.6 3.4 bitcast_dynamic-update-slice_fusion.6
  525.0 3.5 bitcast_dynamic-update-slice_fusion.5
  528.6 3.4 bitcast_dynamic-update-slice_fusion.4
  532.0 3.5 bitcast_dynamic-update-slice_fusion.3
  535.5 4.0 bitcast_dynamic-update-slice_fusion.2
  539.5 3.5 bitcast_dynamic-update-slice_fusion.1
  543.0 3.5 bitcast_dynamic-update-slice_fusion
  546.4 11.8 %convolution_bitcast_fusion = f32[4,8,384,128]{3,1,2,0:T(8,128)S(1)} fusion(bf16[288,49152]{1,0:T(8,128)(2,1)} %bitcast_dynamic-update-slice_fusion, bf16[32,288]{0,1:T(8,128)(2,1)S(1)} %bitcast.197), kind=kOutput, calls=%fused_computation.32 | convolution fusion | flops 905969664 | bytes 34621440 | tf_op jit(solution)/shard_map/dot_general | solution.py:219
  559.4 6.8 fusion.27
  566.2 14.4 %pad.16 = f32[32,384,512]{2,1,0:T(8,128)} pad(f32[32,384,128]{2,1,0:T(8,128)} %get-tuple-element.27, f32[]{:T(128)} %constant.90.clone.1), padding=0_0x0_0x0_384 | pad | bytes 31457284 | tf_op jit(solution)/shard_map/jit(_pad)/pad | solution.py:79
  580.6 21.9 %copy.143 = f32[4,8,384,512]{3,1,2,0:T(8,128)S(1)} copy(f32[4,8,384,512]{3,2,1,0:T(8,128)} %bitcast.164) | data formatting | bytes 50331648
  602.6 8.6 slice.118
  611.2 43.9 %reshape.230 = f32[32,384,511]{2,1,0:T(8,128)} reshape(f32[32,196224]{1,0:T(8,128)} %slice.118) | data formatting | bytes 50233344 | tf_op jit(solution)/shard_map/reshape | solution.py:81
  655.1 10.0 %reduce_sum.77 = f32[32,511]{1,0:T(8,128)S(1)} reduce(f32[32,384,511]{2,1,0:T(8,128)} %reshape.230, f32[]{:T(128)} %constant.90.clone.1), dimensions={1}, to_apply=%region_11.13 | reduce | flops 6262816 | bytes 25182084 | tf_op jit(solution)/shard_map/reduce_sum | solution.py:81
  667.3 13.6 %fusion.35 = f32[9,32,32]{2,1,0:T(8,128)S(1)} fusion(bf16[9,32,49152]{2,1,0:T(8,128)(2,1)} %bitcast.26, bf16[32,49152,1]{1,0,2:T(8,128)(2,1)} %reshape.256), kind=kOutput, calls=%fused_computation.110 | convolution fusion | flops 905969664 | bytes 31494144 | tf_op jit(solution)/shard_map/dot_general | solution.py:196
  680.9 133.0 %all-reduce.5 = (f32[]{:T(128)}, f32[9,32,32]{2,1,0:T(8,128)S(1)}) all-reduce(f32[]{:T(128)} %get-tuple-element.58, f32[9,32,32]{2,1,0:T(8,128)S(1)} %fusion.35), channel_id=1, replica_groups=mesh['enc'=8,'bin'=16,'off'=2] {'bin','off'}, use_global_device_ids=true, to_apply=%region_3.4 | all-reduce | flops 9217 | bytes 73736 | tf_op jit(solution)/shard_map/psum | solution.py:231
  814.0 66.4 %all-reduce.11 = (f32[]{:T(128)}, f32[9,32,32]{2,1,0:T(8,128)}, bf16[2,32,6144]{2,1,0:T(8,128)(2,1)S(1)}) all-reduce(f32[]{:T(128)} %get-tuple-element.21, f32[9,32,32]{2,1,0:T(8,128)S(1)} %get-tuple-element.22, f32[2,32,6144]{2,1,0:T(8,128)} %all-reduce.10.cloned.1.call-done), channel_id=1, replica_groups=mesh['enc'=8,'bin'=16,'off'=2] {'enc'}, use_global_device_ids=true, to_apply=%region_4.5 | all-reduce | flops 402433 | bytes 2433032 | tf_op jit(solution)/shard_map/psum | solution.py:230
  881.3 5.4 all-to-all-start.2
  888.7 4.6 all-to-all-done.2
  893.3 4.7 all-to-all-start.3
  900.6 4.7 all-to-all-done.3
  (164 shorter events, 67.4 us)
Async XLA Ops:
  7.2 35.4 %copy-start.31 = (bf16[16,768]{1,0:T(8,128)(2,1)S(1)}, bf16[16,768]{1,0:T(8,128)(2,1)}, u32[]{:S(2)}) copy-start(bf16[16,768]{1,0:T(8,128)(2,1)} %param.12) | copy-start | bytes 73732
  8.2 5.8 collective-permute-start.1
  11.9 5.5 collective-permute-start
  18.5 22.0 %all-to-all-start = ((bf16[32,16,784]{2,1,0:T(8,128)(2,1)}), bf16[32,16,784]{2,1,0:T(8,128)(2,1)S(1)}, u32[]{:S(2)}, u32[]{:S(2)}) async-start(bf16[32,16,784]{2,1,0:T(8,128)(2,1)} %broadcast_in_dim.26), calls=%async_computation | async-start | bytes 1835008 | tf_op jit(solution)/shard_map/all_to_all | solution.py:28
  24.1 111.5 %all-gather.3.cloned.1.call-start = ((), (), s32[]{:S(2)}) async-start(), calls=%async_computation.5 | async-start | bytes 6488064 | tf_op jit(solution)/shard_map/all_gather | solution.py:45
  41.7 0.9 copy-start.16
  41.7 1.3 copy-start.18
  41.7 1.4 copy-start.20
  42.6 104.6 %copy-start.30 = (s32[6144]{0:T(1024)S(1)}, s32[6144]{0:T(1024)}, u32[]{:S(2)}) copy-start(s32[6144]{0:T(1024)} %param.19) | copy-start | bytes 73732
  42.6 105.3 %copy-start.27 = (s32[6144]{0:T(1024)S(1)}, s32[6144]{0:T(1024)}, u32[]{:S(2)}) copy-start(s32[6144]{0:T(1024)} %param.20) | copy-start | bytes 73732
  43.1 0.6 copy-start.28
  139.7 76.8 %all-to-all-start.1 = ((bf16[8,64,768]{2,1,0:T(8,128)(2,1)}), bf16[8,64,768]{2,1,0:T(8,128)(2,1)S(1)}, u32[]{:S(2)}, u32[]{:S(2)}) async-start(bf16[8,64,768]{2,1,0:T(8,128)(2,1)} %broadcast_in_dim.27), calls=%async_computation.1 | async-start | bytes 1572864 | tf_op jit(solution)/shard_map/all_to_all | solution.py:28
  147.2 666.8 %all-reduce.10.cloned.1.call-start = ((), (), s32[]{:S(2)}) async-start(), calls=%async_computation.4 | async-start | bytes 3145728 | tf_op jit(solution)/shard_map/psum | solution.py:231
  261.1 4.6 copy-start.1
  267.6 5.1 collective-permute-start.3
  268.9 3.9 collective-permute-start.2
  272.8 4.1 copy-start.26
  280.9 34.8 %collective-permute-start.5 = (bf16[32,400,8]{1,2,0:T(8,128)(2,1)}, bf16[32,400,8]{1,2,0:T(8,128)(2,1)}, u32[]{:S(2)}, u32[]{:S(2)}) collective-permute-start(bf16[32,400,8]{1,2,0:T(8,128)(2,1)} %copy.102), channel_id=1, source_target_pairs={{1,0},{32,1},{33,32},{64,33},{65,64},{96,65},{97,96},{128,97},{129... | collective-permute-start | bytes 614408 | tf_op jit(solution)/shard_map/ppermute | solution.py:19
  288.2 31.1 %collective-permute-start.4 = (bf16[32,400,8]{1,2,0:T(8,128)(2,1)}, bf16[32,400,8]{1,2,0:T(8,128)(2,1)}, u32[]{:S(2)}, u32[]{:S(2)}) collective-permute-start(bf16[32,400,8]{1,2,0:T(8,128)(2,1)} %copy.101), channel_id=1, source_target_pairs={{0,1},{1,32},{32,33},{33,64},{64,65},{65,96},{96,97},{97,128},{128... | collective-permute-start | bytes 614408 | tf_op jit(solution)/shard_map/ppermute | solution.py:17
  369.8 5.5 copy-start.14
  369.8 9.0 copy-start.12
  375.3 6.9 copy-start.10
  382.3 7.2 copy-start.8
  385.9 7.1 copy-start.6
  389.4 7.4 copy-start.4
  392.9 7.4 copy-start.2
  396.8 7.0 copy-start.24
  415.6 3.7 copy-start.35
  416.7 2.6 copy-start
  419.3 4.3 copy-start.22
  419.3 4.3 copy-start.32
  419.3 4.3 copy-start.33
  419.3 4.3 copy-start.36
  423.5 6.9 copy-start.23
  430.5 4.8 collective-permute-start.7
  431.8 4.4 collective-permute-start.6
  440.2 16.3 %copy-start.25 = (bf16[9,32,32]{2,1,0:T(8,128)(2,1)S(1)}, bf16[9,32,32]{2,1,0:T(8,128)(2,1)}, u32[]{:S(2)}) copy-start(bf16[9,32,32]{2,1,0:T(8,128)(2,1)} %param.16) | copy-start | bytes 55300
  444.3 15.1 %collective-permute-start.9 = (bf16[32,400,8]{1,2,0:T(8,128)(2,1)}, bf16[32,400,8]{1,2,0:T(8,128)(2,1)}, u32[]{:S(2)}, u32[]{:S(2)}) collective-permute-start(bf16[32,400,8]{1,2,0:T(8,128)(2,1)} %copy.110), channel_id=1, source_target_pairs={{1,0},{32,1},{33,32},{64,33},{65,64},{96,65},{97,96},{128,97},{129... | collective-permute-start | bytes 614408 | tf_op jit(solution)/shard_map/ppermute | solution.py:19
  452.1 10.9 %collective-permute-start.8 = (bf16[32,400,8]{1,2,0:T(8,128)(2,1)}, bf16[32,400,8]{1,2,0:T(8,128)(2,1)}, u32[]{:S(2)}, u32[]{:S(2)}) collective-permute-start(bf16[32,400,8]{1,2,0:T(8,128)(2,1)} %copy.109), channel_id=1, source_target_pairs={{0,1},{1,32},{32,33},{33,64},{64,65},{65,96},{96,97},{97,128},{128... | collective-permute-start | bytes 614408 | tf_op jit(solution)/shard_map/ppermute | solution.py:17
  512.6 5.5 copy-start.15
  512.6 9.0 copy-start.13
  518.1 6.9 copy-start.11
  525.0 7.0 copy-start.9
  528.6 7.0 copy-start.7
  532.0 7.5 copy-start.5
  535.5 7.5 copy-start.3
  667.3 213.1 %copy-start.29 = (bf16[16,768]{1,0:T(8,128)(2,1)S(1)}, bf16[16,768]{1,0:T(8,128)(2,1)}, u32[]{:S(2)}) copy-start(bf16[16,768]{1,0:T(8,128)(2,1)} %copy-done.28) | copy-start | bytes 73732
  667.3 219.5 %copy-start.17 = (bf16[512,768]{1,0:T(8,128)(2,1)S(1)}, bf16[512,768]{1,0:T(8,128)(2,1)}, u32[]{:S(2)}) copy-start(bf16[512,768]{1,0:T(8,128)(2,1)} %copy-done.16) | copy-start | bytes 2359300
  667.3 219.5 %copy-start.19 = (bf16[512,768]{1,0:T(8,128)(2,1)S(1)}, bf16[512,768]{1,0:T(8,128)(2,1)}, u32[]{:S(2)}) copy-start(bf16[512,768]{1,0:T(8,128)(2,1)} %copy-done.18) | copy-start | bytes 2359300
  667.3 219.5 %copy-start.21 = (bf16[512,768]{1,0:T(8,128)(2,1)S(1)}, bf16[512,768]{1,0:T(8,128)(2,1)}, u32[]{:S(2)}) copy-start(bf16[512,768]{1,0:T(8,128)(2,1)} %copy-done.20) | copy-start | bytes 2359300
  667.3 219.5 %copy-start.34 = (bf16[2,16,32]{2,1,0:T(8,128)(2,1)S(1)}, bf16[2,16,32]{2,1,0:T(8,128)(2,1)}, u32[]{:S(2)}) copy-start(bf16[2,16,32]{2,1,0:T(8,128)(2,1)} %param.15) | copy-start | bytes 6148
  881.3 12.0 %all-to-all-start.2 = ((f32[8,1,1024]{2,1,0:T(1,128)}), f32[8,1,1024]{2,1,0:T(1,128)S(1)}, u32[]{:S(2)}, u32[]{:S(2)}) async-start(f32[8,1,1024]{2,1,0:T(1,128)} %reshape.268), calls=%async_computation.2 | async-start | bytes 65536 | tf_op jit(solution)/shard_map/all_to_all | solution.py:28
  893.3 12.0 %all-to-all-start.3 = ((f32[8,1,3072]{2,1,0:T(1,128)}), f32[8,1,3072]{2,1,0:T(1,128)S(1)}, u32[]{:S(2)}, u32[]{:S(2)}) async-start(f32[8,1,3072]{2,1,0:T(1,128)} %reshape.270), calls=%async_computation.3 | async-start | bytes 196608 | tf_op jit(solution)/shard_map/all_to_all | solution.py:61
Sparse Core Ops, SparseCore 0:
  44.8 90.7 all-gather.2
  667.4 130.9 all-reduce.9
